TPU v7x, 32 devices: a whole 2x2x4 slice. The times are simulated.
32 devices in a mesh: fsdp: 2 (over core), ctx: 4 (over y, x), tp: 4 (over z).
Axes of the slice: x: 2, y: 2, z: 4, core: 2. Of those that a mesh axis runs over, the one named last changes fastest.
Arguments:
- tokens_in: bfloat16 [4, 2048, 768], P(None, ('fsdp', 'ctx', 'tp')), may hold values from -6 to 6
- cotangent: bfloat16 [4, 2048, 768], P(None, ('fsdp', 'ctx', 'tp')), may hold values from -6 to 6
- seq_lengths: int32 [4, 2, 3], P(None, 'fsdp'), may hold values from 1 to 512, 1024 in all within a row
- row_order: int32 [4, 2, 1024], P(None, 'fsdp'), may hold values from 0 to 1023, each once within a row
- w_query: bfloat16 [768, 768], P(('fsdp', 'ctx'), 'tp'), may hold values from -0.3125 to 0.3125
- b_query: bfloat16 [12, 64], P('tp', ('fsdp', 'ctx')), may hold values from -3 to 3
- w_key: bfloat16 [768, 768], P(('fsdp', 'ctx'), 'tp'), may hold values from -0.3125 to 0.3125
- w_value: bfloat16 [768, 768], P(('fsdp', 'ctx'), 'tp'), may hold values from -0.21875 to 0.21875
- b_value: bfloat16 [12, 64], P('tp', ('fsdp', 'ctx')), may hold values from -3 to 3
- w_out: bfloat16 [768, 768], P(('fsdp', 'ctx'), 'tp'), may hold values from -1 to 1
- b_out: bfloat16 [768], P(('fsdp', 'ctx')), may hold values from -3 to 3
- mid_gain: bfloat16 [768], P(('fsdp', 'ctx')), may hold values from 0.099609375 to 1.8984375
- mid_shift: bfloat16 [768], P(('fsdp', 'ctx')), may hold values from -3 to 3
- w_up: bfloat16 [768, 3072], P(('fsdp', 'ctx'), 'tp'), may hold values from -0.21875 to 0.21875
- b_up: bfloat16 [12, 256], P('tp', ('fsdp', 'ctx')), may hold values from -3 to 3
- w_down: bfloat16 [768, 3072], P(('fsdp', 'ctx'), 'tp'), may hold values from -0.15625 to 0.15625
- b_down: bfloat16 [768], P(('fsdp', 'ctx')), may hold values from -3 to 3
- end_gain: bfloat16 [768], P(('fsdp', 'ctx')), may hold values from 0.099609375 to 1.8984375
- end_shift: bfloat16 [768], P(('fsdp', 'ctx')), may hold values from -3 to 3
Outputs:
- layer_out: bfloat16 [4, 2048, 768], P(None, ('fsdp', 'ctx', 'tp'))
- input_grad: bfloat16 [4, 2048, 768], P(None, ('fsdp', 'ctx', 'tp'))
- grad_w_query: float32 [768, 768], P(('fsdp', 'ctx'), 'tp')
- grad_b_query: float32 [12, 64], P('tp', ('fsdp', 'ctx'))
- grad_w_key: float32 [768, 768], P(('fsdp', 'ctx'), 'tp')
- grad_w_value: float32 [768, 768], P(('fsdp', 'ctx'), 'tp')
- grad_b_value: float32 [12, 64], P('tp', ('fsdp', 'ctx'))
- grad_w_out: float32 [768, 768], P(('fsdp', 'ctx'), 'tp')
- grad_b_out: float32 [768], P(('fsdp', 'ctx'))
- grad_mid_gain: float32 [768], P(('fsdp', 'ctx'))
- grad_mid_shift: float32 [768], P(('fsdp', 'ctx'))
- grad_w_up: float32 [768, 3072], P(('fsdp', 'ctx'), 'tp')
- grad_b_up: float32 [12, 256], P('tp', ('fsdp', 'ctx'))
- grad_w_down: float32 [768, 3072], P(('fsdp', 'ctx'), 'tp')
- grad_b_down: float32 [768], P(('fsdp', 'ctx'))
- grad_end_gain: float32 [768], P(('fsdp', 'ctx'))
- grad_end_shift: float32 [768], P(('fsdp', 'ctx'))
Inputs may be any that keep to these rules, and one draw needn't show every extreme that they name: `seq_lengths`: each row of 3 lengths sums to 1024, and its largest is exactly 512. `row_order`: each row holds every number of 0 to 1023 once.
All inputs are finite; a program needn't handle non-finite values.
Results may differ from a plain program's by a relative error of at most 0.02.
Values may be sent and summed in bfloat16 or wider, within the bound.
A program may use at most 128 MiB of HBM per device.

v0:
```python
import jax
import jax.numpy as jnp
from jax import lax
from jax.sharding import PartitionSpec as P

EPS = 1e-06
MASKED = -1e30
ALL = ("fsdp", "ctx", "tp")
ROWS = ("fsdp", "ctx")
BF = jnp.bfloat16
F32 = jnp.float32


def mm(a, b):
    return jnp.dot(a, b, preferred_element_type=F32)


def mm_rt(a, b):
    return lax.dot_general(a, b, (((1,), (1,)), ((), ())), preferred_element_type=F32)


def mm_lt(a, b):
    return lax.dot_general(a, b, (((0,), (0,)), ((), ())), preferred_element_type=F32)


def norm(u):
    centre = u - jnp.mean(u, axis=-1, keepdims=True)
    inv = lax.rsqrt(jnp.mean(centre * centre, axis=-1, keepdims=True) + EPS)
    return (centre * inv, inv)


def norm_back(d, gain, n, inv):
    e = d * gain
    return (
        e - jnp.mean(e, axis=-1, keepdims=True) - n * jnp.mean(e * n, axis=-1, keepdims=True)
    ) * inv


def phi_both(u):
    cdf = 0.5 * (1.0 + lax.erf(u * 0.7071067811865476))
    pdf = 0.3989422804014327 * jnp.exp(-0.5 * u * u)
    return (cdf, pdf)


def gather_group(block):
    width = block.shape[-1]
    mine = lax.all_to_all(block, "ctx", 0, 0, tiled=True)
    whole = lax.all_gather(mine, "tp", axis=1, tiled=False)
    return whole.reshape(-1, width)


def scatter_group(rows, own_rows):
    ctx_n, tp_n = (lax.axis_size("ctx"), lax.axis_size("tp"))
    width = rows.shape[-1]
    blocks = rows.reshape(ctx_n, tp_n * own_rows, width)
    mine = lax.psum_scatter(blocks, "tp", scatter_dimension=1, tiled=True)
    return lax.all_to_all(mine, "ctx", 0, 0, tiled=True)


def body(
    tokens_in,
    cotangent,
    seq_lengths,
    row_order,
    w_query,
    b_query,
    w_key,
    w_value,
    b_value,
    w_out,
    b_out,
    mid_gain,
    mid_shift,
    w_up,
    b_up,
    w_down,
    b_down,
    end_gain,
    end_shift,
):
    ctx_n, tp_n, fsdp_n = (lax.axis_size("ctx"), lax.axis_size("tp"), lax.axis_size("fsdp"))
    rows_n = ctx_n * fsdp_n
    c, t = (lax.axis_index("ctx"), lax.axis_index("tp"))
    micro, own_rows, width = tokens_in.shape
    group_rows = own_rows * ctx_n * tp_n
    half_rows = group_rows // 2
    parts = tp_n // 2
    my_rows = half_rows // parts
    half, quarter = (t // parts, t % parts)
    heads_l, head_l = b_query.shape
    heads, head = (heads_l * tp_n, head_l * rows_n)
    mats = (w_query, w_key, w_value, w_out, w_up, w_down)
    widths = [m.shape[1] for m in mats]
    packed = lax.all_gather(jnp.concatenate(mats, axis=1), ALL, axis=0, tiled=False)
    full, at = ([], 0)
    for wd in widths:
        piece = packed[:, :, at : at + wd].reshape(rows_n, tp_n, -1, wd)
        full.append(piece.transpose(0, 2, 1, 3).reshape(width, tp_n * wd))
        at += wd
    wq, wk, wv, wo, wu, wd_ = full
    vecs = (b_out, mid_gain, mid_shift, b_down, end_gain, end_shift)
    bias = (b_query, b_value, b_up)
    vec_all = lax.all_gather(jnp.stack(vecs), ROWS, axis=1, tiled=True).astype(F32)
    bias_all = lax.all_gather(jnp.concatenate(bias, axis=1), ALL, axis=0, tiled=False).astype(F32)

    def whole_bias(at, wd):
        piece = bias_all[:, :, at : at + wd].reshape(rows_n, tp_n, heads_l, wd)
        return piece.transpose(1, 2, 0, 3).reshape(-1)

    bq = whole_bias(0, head_l)
    bv = whole_bias(head_l, head_l)
    bu = whole_bias(2 * head_l, b_up.shape[1])
    bo, mg, ms, bd, eg, es = (vec_all[i] for i in range(6))
    lens = lax.dynamic_index_in_dim(seq_lengths[:, 0], c, 0, keepdims=False)
    order = lax.dynamic_index_in_dim(row_order[:, 0], c, 0, keepdims=False)
    places = lax.iota(jnp.int32, lens.shape[0])
    longest = jnp.argmax(lens)
    first = jnp.sum(jnp.where(places < longest, lens, 0))
    start = lax.rem(first + half * half_rows, group_rows)
    ends = jnp.cumsum(lens)
    nat = lax.rem(start + lax.iota(jnp.int32, half_rows), group_rows)
    seg = jnp.sum((ends[None, :] <= nat[:, None]).astype(jnp.int32), axis=1)
    q_at = quarter * my_rows
    nat_q = lax.dynamic_slice_in_dim(nat, q_at, my_rows)
    seg_q = lax.dynamic_slice_in_dim(seg, q_at, my_rows)
    x_group = gather_group(tokens_in)
    c_group = gather_group(cotangent)
    x_twice = jnp.concatenate([x_group, x_group[:half_rows]], axis=0)
    x_half = lax.dynamic_slice_in_dim(x_twice, start, half_rows, 0)
    x_mine = lax.dynamic_slice_in_dim(x_half, q_at, my_rows, 0)
    pick = (order[:, None] == nat_q[None, :]).astype(BF)
    pick_nat = (lax.iota(jnp.int32, group_rows)[:, None] == nat_q[None, :]).astype(BF)
    dy = mm_lt(pick, c_group)
    x = x_mine.astype(F32)
    q = (mm(x_mine, wq) + bq).astype(BF).reshape(my_rows, heads, head)
    k = mm(x_half, wk).astype(BF).reshape(half_rows, heads, head)
    v = (mm(x_half, wv) + bv).astype(BF).reshape(half_rows, heads, head)
    same = seg_q[:, None] == seg[None, :]
    s = jnp.einsum("qhd,khd->hqk", q, k, preferred_element_type=F32) * 0.125
    s = jnp.where(same[None], s, MASKED)
    p = jnp.exp(s - jnp.max(s, axis=-1, keepdims=True))
    p = p / jnp.sum(p, axis=-1, keepdims=True)
    pb = p.astype(BF)
    o = jnp.einsum("hqk,khd->qhd", pb, v, preferred_element_type=F32).astype(BF)
    o2 = o.reshape(my_rows, heads * head)
    r1 = x + mm_rt(o2, wo) + bo
    n1, inv1 = norm(r1)
    middle = n1 * mg + ms
    mid_b = middle.astype(BF)
    pre = mm(mid_b, wu) + bu
    cdf, pdf = phi_both(pre)
    act = (pre * cdf).astype(BF)
    r2 = middle + mm_rt(act, wd_) + bd
    n2, inv2 = norm(r2)
    y = n2 * eg + es
    d_r2 = norm_back(dy, eg, n2, inv2)
    df = d_r2.astype(BF)
    d_pre = (mm(df, wd_) * (cdf + pre * pdf)).astype(BF)
    g_down = mm_lt(df, act)
    g_up = mm_lt(mid_b, d_pre)
    d_mid = d_r2 + mm_rt(d_pre, wu)
    d_r1 = norm_back(d_mid, mg, n1, inv1)
    da = d_r1.astype(BF)
    g_out = mm_lt(da, o2)
    d_o = mm(da, wo).astype(BF).reshape(my_rows, heads, head)
    dp = jnp.einsum("qhd,khd->hqk", d_o, v, preferred_element_type=F32)
    ds = (p * (dp - jnp.sum(p * dp, axis=-1, keepdims=True))).astype(BF)
    d_q = (jnp.einsum("hqk,khd->qhd", ds, k, preferred_element_type=F32) * 0.125).astype(BF)
    d_k = jnp.einsum("hqk,qhd->khd", ds, q, preferred_element_type=F32) * 0.125
    d_v = jnp.einsum("hqk,qhd->khd", pb, d_o, preferred_element_type=F32)
    d_q = d_q.reshape(my_rows, heads * head)
    d_kv = jnp.concatenate([d_k.reshape(half_rows, -1), d_v.reshape(half_rows, -1)], axis=1).astype(
        BF
    )
    pairs = [[h * parts + j for j in range(parts)] for h in range(tp_n // parts)]
    d_kv = lax.psum_scatter(
        d_kv.astype(F32), "tp", scatter_dimension=0, tiled=True, axis_index_groups=pairs
    )
    d_k, d_v = jnp.split(d_kv.astype(BF), 2, axis=1)
    g_q = mm_lt(x_mine, d_q)
    g_k = mm_lt(x_mine, d_k)
    g_v = mm_lt(x_mine, d_v)
    d_x = (d_r1 + mm_rt(d_q, wq) + mm_rt(d_k, wk) + mm_rt(d_v, wv)).astype(BF)
    layer_out = scatter_group(mm(pick, y.astype(BF)).astype(BF), own_rows)
    input_grad = scatter_group(mm(pick_nat, d_x).astype(BF), own_rows)
    outs = []
    for g, wd in zip((g_q, g_k, g_v, g_out, g_up, g_down), widths):
        outs.append(g.astype(BF).reshape(rows_n, width // rows_n, tp_n, wd).transpose(0, 2, 1, 3))
    packed_g = jnp.concatenate(outs, axis=3)
    packed_g = packed_g.reshape(rows_n * tp_n, width // rows_n, -1)
    mine_g = lax.psum_scatter(packed_g, ALL, scatter_dimension=0, tiled=True)[0].astype(F32)
    gm, at = ([], 0)
    for wd in widths:
        gm.append(mine_g[:, at : at + wd])
        at += wd

    def total(a):
        return jnp.sum(a.astype(F32), axis=0)

    def split_bias(a, wd):
        return (
            a.reshape(tp_n, heads_l, rows_n, wd)
            .transpose(2, 0, 1, 3)
            .reshape(rows_n * tp_n, heads_l, wd)
        )

    small_b = jnp.concatenate(
        [
            split_bias(total(d_q), head_l),
            split_bias(total(d_v), head_l),
            split_bias(total(d_pre), b_up.shape[1]),
        ],
        axis=2,
    ).reshape(rows_n * tp_n, -1)
    vec_g = jnp.stack(
        [total(d_r1), total(d_mid * n1), total(d_mid), total(d_r2), total(dy * n2), total(dy)]
    )
    small_v = vec_g.reshape(6, rows_n, 1, width // rows_n).transpose(1, 2, 0, 3)
    small_v = jnp.broadcast_to(small_v, (rows_n, tp_n, 6, width // rows_n)).reshape(
        rows_n * tp_n, -1
    )
    small = jnp.concatenate([small_b, small_v], axis=1)
    small = lax.psum_scatter(small, ALL, scatter_dimension=0, tiled=True)[0]
    nb = small_b.shape[1]
    sb = small[:nb].reshape(heads_l, -1)
    sv = small[nb:].reshape(6, -1)
    return (
        layer_out,
        input_grad,
        gm[0],
        sb[:, :head_l],
        gm[1],
        gm[2],
        sb[:, head_l : 2 * head_l],
        gm[3],
        sv[0],
        sv[1],
        sv[2],
        gm[4],
        sb[:, 2 * head_l :],
        gm[5],
        sv[3],
        sv[4],
        sv[5],
    )


def specs():
    tok = P(None, ALL, None)
    grp = P(None, "fsdp", None)
    mat = P(ROWS, "tp")
    bias = P("tp", ROWS)
    vec = P(ROWS)
    ins = (
        tok,
        tok,
        grp,
        grp,
        mat,
        bias,
        mat,
        mat,
        bias,
        mat,
        vec,
        vec,
        vec,
        mat,
        bias,
        mat,
        vec,
        vec,
        vec,
    )
    return (ins, (tok, tok) + ins[4:])


def solution(mesh):
    ins, outs = specs()
    return jax.shard_map(body, mesh=mesh, in_specs=ins, out_specs=outs, check_vma=False)
```

profile of v0, /device:TPU:0, one launch (start us, length us, event | category | flops | bytes accessed | tf_op | source)
XLA Modules:
  0.0 708.5 jit_solution(12837532554560193029)
XLA Ops:
  7.4 13.0 %all_to_all.20 = bf16[4,64,768]{2,1,0:T(8,128)(2,1)} all-to-all(bf16[4,64,768]{2,1,0:T(8,128)(2,1)} %param.19), channel_id=1, replica_groups=mesh['fsdp'=2,'ctx'=4,'tp'=4] {'ctx'}, dimensions={0} | all-to-all | bytes 786432 | tf_op jit(solution)/shard_map/all_to_all | solution.py:47
  29.6 21.1 %all-gather.5 = bf16[8,96,6]{1,2,0:T(8,128)(2,1)S(1)} all-gather(bf16[1,96,6]{1,2,0:T(8,128)(2,1)S(1)} %bitcast.231), channel_id=1, replica_groups=mesh['fsdp'=2,'ctx'=4,'tp'=4] {'fsdp','ctx'}, dimensions={0}, use_global_device_ids=true | all-gather | bytes 10368 | tf_op jit(solution)/shard_map/all_gather | solution.py:103
  50.9 68.8 %all-gather.4 = bf16[32,3,48]{2,1,0:T(4,128)(2,1)S(1)} all-gather(bf16[1,3,48]{2,1,0:T(4,128)(2,1)S(1)} %maximum_bitcast_fusion), channel_id=4, replica_groups=mesh['fsdp'=2,'ctx'=4,'tp'=4] {'fsdp','ctx','tp'}, dimensions={0}, use_global_device_ids=true | all-gather | bytes 9504 | tf_op jit(solution)/shard_map/all_gather | solution.py:104
  128.7 33.1 %all-gather.12.cloned.1.call-done = bf16[3072,2304]{1,0:T(8,128)(2,1)} async-done(((bf16[96,2304]{1,0:T(8,128)(2,1)}), bf16[3072,2304]{1,0:T(8,128)(2,1)}) %all-gather.12.cloned.1.call-update) | async-done | bytes 14155792 | tf_op jit(solution)/shard_map/all_gather | solution.py:94
  161.9 8.1 %fusion.61 = (bf16[32,96,768]{2,1,0:T(8,128)(2,1)}, bf16[32,96,768]{2,1,0:T(8,128)(2,1)}) fusion(bf16[32,96,2304]{2,1,0:T(8,128)(2,1)} %bitcast.177), kind=kLoop, calls=%fused_computation.141 | loop fusion | bytes 18874368 | tf_op jit(solution)/shard_map/slice | solution.py:97
  170.0 7.0 fusion.62
  179.8 3.8 reshape.317
  192.3 3.8 reshape.323
  216.3 6.1 fusion.67
  222.5 4.1 fusion.25
  234.0 14.7 %copy.123 = bf16[8,96,4,768]{3,2,1,0:T(4,128)(2,1)S(1)} copy(bf16[8,96,4,768]{3,1,2,0:T(8,128)(2,1)S(1)} %bitcast.173) | data formatting | bytes 9437184 | tf_op jit(solution)/shard_map/transpose | solution.py:98
  250.1 3.7 multiply_convert_fusion.1
  259.9 5.0 convert_reduce_fusion
  269.7 4.0 multiply_reduce_fusion
  306.3 19.4 %reduce-scatter.7.cloned.1.call-done = f32[256,1536]{0,1:T(8,128)} async-done(((f32[512,1536]{0,1:T(8,128)}), f32[256,1536]{0,1:T(8,128)}) %reduce-scatter.7.cloned.1.call-update) | async-done | bytes 1572880 | tf_op jit(solution)/shard_map/reduce_scatter | solution.py:176
  329.9 3.9 convolution_convert_fusion.2
  335.7 4.4 reshape.344
  341.8 4.4 reshape.347
  346.2 5.2 convolution_convert_fusion.1
  351.4 9.9 %reshape.348 = bf16[8,96,4,768]{3,2,1,0:T(4,128)(2,1)} reshape(bf16[768,3072]{1,0:T(8,128)(2,1)} %convolution_convert_fusion.1) | data formatting | bytes 9437184 | tf_op jit(solution)/shard_map/reshape | solution.py:188
  361.3 3.7 convolution_convert_fusion
  365.0 9.8 %reshape.349 = bf16[8,96,4,768]{3,2,1,0:T(4,128)(2,1)} reshape(bf16[768,3072]{1,0:T(8,128)(2,1)} %convolution_convert_fusion) | data formatting | bytes 9437184 | tf_op jit(solution)/shard_map/reshape | solution.py:188
  376.3 4.5 reshape.345
  382.4 4.8 reshape.346
  387.2 41.3 %concatenate.27 = bf16[8,4,96,2304]{3,1,2,0:T(4,128)(2,1)} concatenate(bf16[8,4,96,192]{3,1,2,0:T(4,128)(2,1)S(1)} %bitcast.179, bf16[8,4,96,192]{3,1,2,0:T(4,128)(2,1)} %bitcast.181, bf16[8,4,96,192]{3,1,2,0:T(4,128)(2,1)} %bitcast.182, bf16[8,4,96,192]{3,1,2,0:T(4,128)(2,1)S(1)} %bitcast.180, bf16[8,4,96,768]{3,1,2,0:T(4,128)(2,1)} %bitcast.167, bf16[8,4,96,768]{3,1,2,0:T(4,128)(2,1)} %bitcast.168), dimensions={3} | concatenate | bytes 28311552 | tf_op jit(solution)/shard_map/concatenate | solution.py:189
  428.5 11.3 %copy.125 = bf16[8,4,96,2304]{3,2,1,0:T(8,128)(2,1)} copy(bf16[8,4,96,2304]{3,1,2,0:T(4,128)(2,1)} %concatenate.27) | data formatting | bytes 28311552 | tf_op jit(solution)/shard_map/concatenate | solution.py:189
  443.5 6.5 all-to-all-done.1
  450.0 40.8 %all-reduce.3.cloned.1.call-done = f32[32,720]{1,0:T(8,128)} async-done(((f32[32,720]{1,0:T(8,128)}), f32[32,720]{1,0:T(8,128)}) %all-reduce.3.cloned.1.call-update) | async-done | bytes 92176
  492.3 37.2 %reduce-scatter.9.cloned.1.call-done = bf16[4,64,768]{2,1,0:T(8,128)(2,1)} async-done(((bf16[4,256,768]{2,1,0:T(8,128)(2,1)}), bf16[4,64,768]{2,1,0:T(8,128)(2,1)}) %reduce-scatter.9.cloned.1.call-update) | async-done | bytes 393232 | tf_op jit(solution)/shard_map/reduce_scatter | solution.py:56
  529.5 3.6 all-to-all-start.3
  535.2 4.1 all-to-all-done.3
  539.4 157.6 %reduce-scatter.11.cloned.1.call-done = bf16[1,96,2304]{2,1,0:T(8,128)(2,1)} async-done(((bf16[32,96,2304]{2,1,0:T(8,128)(2,1)}), bf16[1,96,2304]{2,1,0:T(8,128)(2,1)}) %reduce-scatter.11.cloned.1.call-update) | async-done | bytes 442384 | tf_op jit(solution)/shard_map/reduce_scatter | solution.py:191
  (258 shorter events, 123.2 us)
Async XLA Ops:
  7.2 115.8 %copy-start = (s32[4,1,1024]{2,1,0:T(1,128)S(1)}, s32[4,1,1024]{2,1,0:T(1,128)}, u32[]{:S(2)}) copy-start(s32[4,1,1024]{2,1,0:T(1,128)} %param.22) | copy-start | bytes 49156
  7.2 18.8 %copy-start.50 = (s32[4,1,3]{0,1,2:T(1,128)S(1)}, s32[4,1,3]{0,1,2:T(1,128)}, u32[]{:S(2)}) copy-start(s32[4,1,3]{0,1,2:T(1,128)} %param.21) | copy-start | bytes 148
  7.2 22.3 %copy-start.54 = (bf16[96]{0:T(256)(128)(2,1)S(1)}, bf16[96]{0:T(256)(128)(2,1)}, u32[]{:S(2)}) copy-start(bf16[96]{0:T(256)(128)(2,1)} %param.29) | copy-start | bytes 580
  7.2 22.3 %copy-start.55 = (bf16[96]{0:T(256)(128)(2,1)S(1)}, bf16[96]{0:T(256)(128)(2,1)}, u32[]{:S(2)}) copy-start(bf16[96]{0:T(256)(128)(2,1)} %param.30) | copy-start | bytes 580
  7.2 22.3 %copy-start.56 = (bf16[96]{0:T(256)(128)(2,1)S(1)}, bf16[96]{0:T(256)(128)(2,1)}, u32[]{:S(2)}) copy-start(bf16[96]{0:T(256)(128)(2,1)} %param.31) | copy-start | bytes 580
  7.3 22.3 %copy-start.57 = (bf16[96]{0:T(256)(128)(2,1)S(1)}, bf16[96]{0:T(256)(128)(2,1)}, u32[]{:S(2)}) copy-start(bf16[96]{0:T(256)(128)(2,1)} %param.35) | copy-start | bytes 580
  7.3 22.3 %copy-start.58 = (bf16[96]{0:T(256)(128)(2,1)S(1)}, bf16[96]{0:T(256)(128)(2,1)}, u32[]{:S(2)}) copy-start(bf16[96]{0:T(256)(128)(2,1)} %param.36) | copy-start | bytes 580
  7.3 22.3 %copy-start.59 = (bf16[96]{0:T(256)(128)(2,1)S(1)}, bf16[96]{0:T(256)(128)(2,1)}, u32[]{:S(2)}) copy-start(bf16[96]{0:T(256)(128)(2,1)} %param.37) | copy-start | bytes 580
  7.3 43.5 %copy-start.51 = (bf16[3,32]{1,0:T(4,128)(2,1)S(1)}, bf16[3,32]{1,0:T(4,128)(2,1)}, u32[]{:S(2)}) copy-start(bf16[3,32]{1,0:T(4,128)(2,1)} %param.33) | copy-start | bytes 580
  7.3 43.5 %copy-start.52 = (bf16[3,8]{1,0:T(4,128)(2,1)S(1)}, bf16[3,8]{1,0:T(4,128)(2,1)}, u32[]{:S(2)}) copy-start(bf16[3,8]{1,0:T(4,128)(2,1)} %param.27) | copy-start | bytes 148
  7.3 43.5 %copy-start.53 = (bf16[3,8]{1,0:T(4,128)(2,1)S(1)}, bf16[3,8]{1,0:T(4,128)(2,1)}, u32[]{:S(2)}) copy-start(bf16[3,8]{1,0:T(4,128)(2,1)} %param.24) | copy-start | bytes 148
  7.3 117.9 %all-gather.10.cloned.1.call-start = ((), (), s32[]{:S(2)}) async-start(), calls=%async_computation.12 | async-start | bytes 1966080 | tf_op jit(solution)/shard_map/all_gather | solution.py:48
  20.4 141.5 %all-gather.12.cloned.1.call-start = ((), (), s32[]{:S(2)}) async-start(), calls=%async_computation.13 | async-start | bytes 14598144 | tf_op jit(solution)/shard_map/all_gather | solution.py:94
  22.4 101.9 %all-to-all-start.2 = ((bf16[4,64,768]{2,1,0:T(8,128)(2,1)}), bf16[4,64,768]{2,1,0:T(8,128)(2,1)S(1)}, u32[]{:S(2)}, u32[]{:S(2)}) async-start(bf16[4,64,768]{2,1,0:T(8,128)(2,1)} %param.20), calls=%async_computation.3 | async-start | bytes 786432 | tf_op jit(solution)/shard_map/all_to_all | solution.py:47
  25.9 229.8 %all-gather.14.cloned.1.call-start = ((), (), s32[]{:S(2)}) async-start(), calls=%async_computation.14 | async-start | bytes 1966080 | tf_op jit(solution)/shard_map/all_gather | solution.py:48
  125.1 200.6 %reduce-scatter.7.cloned.1.call-start = ((), (), s32[]{:S(2)}) async-start(), calls=%async_computation.9 | async-start | bytes 4718592 | tf_op jit(solution)/shard_map/reduce_scatter | solution.py:176
  227.2 40.0 %copy-start.2 = (f32[256,768]{1,0:T(8,128)}, f32[256,768]{1,0:T(8,128)S(1)}, u32[]{:S(2)}) copy-start(f32[256,768]{1,0:T(8,128)S(1)} %get-tuple-element.62) | copy-start | bytes 2359300
  231.9 18.1 %copy-start.9 = (bf16[96,8,4,768]{3,1,2,0:T(8,128)(2,1)}, bf16[96,8,4,768]{3,1,2,0:T(8,128)(2,1)S(1)}, u32[]{:S(2)}) copy-start(bf16[96,8,4,768]{3,1,2,0:T(8,128)(2,1)S(1)} %copy.130) | copy-start | bytes 14155780
  249.8 17.3 %copy-start.33 = (f32[256]{0:T(256)}, f32[256]{0:T(256)S(1)}, u32[]{:S(2)}) copy-start(f32[256]{0:T(256)S(1)} %broadcast_multiply_fusion.5) | copy-start | bytes 3076
  250.1 17.1 %copy-start.41 = (f32[256]{0:T(256)}, f32[256]{0:T(256)S(1)}, u32[]{:S(2)}) copy-start(f32[256]{0:T(256)S(1)} %add_rsqrt_fusion.1) | copy-start | bytes 3076
  283.5 156.4 %reduce-scatter.5.cloned.1.call-start = ((), (), s32[]{:S(2)}) async-start(), calls=%async_computation.8 | async-start | bytes 1966080 | tf_op jit(solution)/shard_map/reduce_scatter | solution.py:56
  286.7 204.1 %all-reduce.3.cloned.1.call-start = ((), (), s32[]{:S(2)}) async-start(), calls=%async_computation.15 | async-start | bytes 196608
  303.9 23.6 %copy-start.29 = (f32[8,4,3,32]{3,1,0,2:T(4,128)S(1)}, f32[8,4,3,32]{3,1,0,2:T(4,128)}, u32[]{:S(2)}) copy-start(f32[8,4,3,32]{3,1,0,2:T(4,128)} %copy.128) | copy-start | bytes 36868
  304.0 23.7 %copy-start.28 = (f32[32,576]{1,0:T(8,128)S(1)}, f32[32,576]{1,0:T(8,128)}, u32[]{:S(2)}) copy-start(f32[32,576]{1,0:T(8,128)} %reshape.358) | copy-start | bytes 221188
  304.0 24.4 %copy-start.13 = (bf16[768,768]{0,1:T(8,128)(2,1)S(1)}, bf16[768,768]{0,1:T(8,128)(2,1)}, u32[]{:S(2)}) copy-start(bf16[768,768]{0,1:T(8,128)(2,1)} %copy-done.12) | copy-start | bytes 3538948
  306.3 23.7 %copy-start.45 = (s32[256]{0:T(256)S(1)}, s32[256]{0:T(256)}, u32[]{:S(2)}) copy-start(s32[256]{0:T(256)} %dynamic_slice.25) | copy-start | bytes 3076
  329.9 199.6 %reduce-scatter.9.cloned.1.call-start = ((), (), s32[]{:S(2)}) async-start(), calls=%async_computation.10 | async-start | bytes 1966080 | tf_op jit(solution)/shard_map/reduce_scatter | solution.py:56
  333.9 363.1 %reduce-scatter.11.cloned.1.call-start = ((), (), s32[]{:S(2)}) async-start(), calls=%async_computation.11 | async-start | bytes 14598144 | tf_op jit(solution)/shard_map/reduce_scatter | solution.py:191
  376.3 10.9 %copy-start.7 = (bf16[8,96,4,192]{3,2,1,0:T(4,128)(2,1)S(1)}, bf16[8,96,4,192]{3,2,1,0:T(4,128)(2,1)}, u32[]{:S(2)}) copy-start(bf16[8,96,4,192]{3,2,1,0:T(4,128)(2,1)} %reshape.344) | copy-start | bytes 3538948
  439.8 261.3 %copy-start.1 = (s32[4,1,1024]{2,1,0:T(1,128)S(1)}, s32[4,1,1024]{2,1,0:T(1,128)}, u32[]{:S(2)}) copy-start(s32[4,1,1024]{2,1,0:T(1,128)} %param.22) | copy-start | bytes 49156
  439.9 10.1 %all-to-all-start.1 = ((bf16[4,64,768]{2,1,0:T(8,128)(2,1)}), bf16[4,64,768]{2,1,0:T(8,128)(2,1)S(1)}, u32[]{:S(2)}, u32[]{:S(2)}) async-start(bf16[4,64,768]{2,1,0:T(8,128)(2,1)} %reduce-scatter.5.cloned.1.call-done), calls=%async_computation.2 | async-start | bytes 786432 | tf_op jit(solution)/shard_map/all_to_all | solution.py:57
  529.5 9.9 %all-to-all-start.3 = ((bf16[4,64,768]{2,1,0:T(8,128)(2,1)}), bf16[4,64,768]{2,1,0:T(8,128)(2,1)S(1)}, u32[]{:S(2)}, u32[]{:S(2)}) async-start(bf16[4,64,768]{2,1,0:T(8,128)(2,1)} %reduce-scatter.9.cloned.1.call-done), calls=%async_computation.6 | async-start | bytes 786432 | tf_op jit(solution)/shard_map/all_to_all | solution.py:57
  (45 other events, 187.0 us)
Sparse Core Ops, SparseCore 0:
  20.5 36.9 all-gather.9
  60.3 101.5 all-gather.11
  163.4 35.4 all-gather.13
  283.6 42.0 reduce-scatter.6
  327.8 35.3 reduce-scatter.4
  369.3 121.4 all-reduce.2
  493.1 36.3 reduce-scatter.8
  535.5 161.4 reduce-scatter.10
where the time goes:
time: 722 us; the launch traced here: 708 us
  waiting for transfers between devices  299 us (41%)
  local copies, waits for them, and re-layouts  189 us (26%)
  blocking collectives  103 us (14%)
  matrix products  73.7 us (10%)
  between operations  16.2 us (2%)
  other arithmetic  15.8 us (2%)
  starting transfers between devices  11.3 us (2%)
    reduce_scatter x1, waiting for transfers between devices, body(): lax.psum_scatter(packed_g, ALL, scatter_dimension=0, tiled=True)[0]  158 us
    all_gather x1, blocking collectives, body(): lax.all_gather(jnp.concatenate(bias, axis=1), ALL, axis=0, tiled=False)  68.8 us
    concatenate x2, local copies, waits for them, and re-layouts, body(): packed_g = jnp.concatenate(outs, axis=3)  52.6 us
    unnamed x9, waiting for transfers between devices  41 us
    reshape x6, local copies, waits for them, and re-layouts, body(): g.astype(BF).reshape(rows_n, width // rows_n, tp_n, wd)  37.8 us
    reduce_scatter x2, waiting for transfers between devices, scatter_group(): mine = lax.psum_scatter(blocks, 'tp', scatter_dimension=1, tiled=True)  37.3 us
    all_gather x1, waiting for transfers between devices, body(): lax.all_gather(jnp.concatenate(mats, axis=1), ALL, axis=0, tiled=False)  33.1 us
    transpose x6, local copies, waits for them, and re-layouts, body(): full.append(piece.transpose(0, 2, 1, 3).reshape(width, tp_n * wd))  27.6 us
  transfers between devices with their start and end apart: 11, of which 7 were waited for; matrix products, arithmetic and copies ran while one was open for 34% of the time, Pallas kernels for 0%

commit v1 on v0

--- a/solution.py
+++ b/solution.py
@@ -1,3 +1,4 @@
+import functools
 import jax
 import jax.numpy as jnp
 from jax import lax
@@ -11,6 +12,40 @@
 F32 = jnp.float32
 
 
+def convert_the_patches(frame_in, array_axis, local_array):
+    b_now = frame_in.shape
+    g_now = frame_in.reshape(
+        *b_now[:array_axis], local_array, b_now[array_axis] // local_array, *b_now[array_axis + 1 :]
+    )
+    return jnp.moveaxis(g_now, array_axis, 0)
+
+
+def lots_all_manage(field, ndim_at):
+    field = jnp.moveaxis(field, 0, ndim_at)
+    aux = field.shape
+    return field.reshape(*aux[:ndim_at], aux[ndim_at] * aux[ndim_at + 1], *aux[ndim_at + 2 :])
+
+
+def wait_sector_in(sample, lane_axis, raw, x_part):
+    m_next = lax.axis_size(lane_axis)
+    out_arr = lax.axis_index(lane_axis)
+    current_arr, plain = (m_next, out_arr)
+    y1 = convert_the_patches(sample, raw, current_arr)
+    src_i = 1
+    series = [y1[plain]]
+    while src_i < current_arr:
+        mid_arr = y1[plain ^ src_i]
+        series.append(
+            lax.ppermute(mid_arr, lane_axis, [(no, no ^ src_i) for no in range(current_arr)])
+        )
+        src_i = src_i + 1
+    y1 = jnp.stack(series)[plain ^ jnp.arange(current_arr)]
+    return lots_all_manage(y1, x_part)
+
+
+_measure_state = functools.partial(wait_sector_in, lane_axis="ctx", raw=0, x_part=0)
+
+
 def mm(a, b):
     return jnp.dot(a, b, preferred_element_type=F32)
 
@@ -44,7 +79,7 @@
 
 def gather_group(block):
     width = block.shape[-1]
-    mine = lax.all_to_all(block, "ctx", 0, 0, tiled=True)
+    mine = _measure_state(block)
     whole = lax.all_gather(mine, "tp", axis=1, tiled=False)
     return whole.reshape(-1, width)
 

time: 722 us -> 704 us (0.975)
  blocking collectives: 103 us -> 89 us
    all_to_all x1 -> x0, blocking collectives: 13 us -> none  [gather_group(): mine = lax.all_to_all(block, 'ctx', 0, 0, tiled=True)]
    transpose x6, local copies, waits for them, and re-layouts: 27.6 us -> 16.8 us  [body(): full.append(piece.transpose(0, 2, 1, 3).reshape(width, tp_n * wd))]
    ppermute x0 -> x6, starting transfers between devices: none -> 8.18 us  [wait_sector_in(): lax.ppermute(mid_arr, lane_axis, [(no, no ^ src_i) for no in range(curren...]
  transfers between devices with their start and end apart: 11 -> 16, of which waited for: 7 -> 10; matrix products, arithmetic and copies ran while one was open for 34% -> 34% of each run, Pallas kernels for 0% -> 0%
where the time goes in v1:
time: 704 us; the launch traced here: 697 us
  waiting for transfers between devices  304 us (43%)
  local copies, waits for them, and re-layouts  182 us (26%)
  blocking collectives  89 us (13%)
  matrix products  73.7 us (10%)
  starting transfers between devices  16.2 us (2%)
  between operations  16.1 us (2%)
  other arithmetic  15.9 us (2%)
    reduce_scatter x1, waiting for transfers between devices, body(): lax.psum_scatter(packed_g, ALL, scatter_dimension=0, tiled=True)[0]  158 us
    all_gather x1, blocking collectives, body(): lax.all_gather(jnp.concatenate(bias, axis=1), ALL, axis=0, tiled=False)  68.4 us
    concatenate x2, local copies, waits for them, and re-layouts, body(): packed_g = jnp.concatenate(outs, axis=3)  52.6 us
    unnamed x9, waiting for transfers between devices  41 us
    reshape x6, local copies, waits for them, and re-layouts, body(): g.astype(BF).reshape(rows_n, width // rows_n, tp_n, wd)  37.8 us
    reduce_scatter x2, waiting for transfers between devices, scatter_group(): mine = lax.psum_scatter(blocks, 'tp', scatter_dimension=1, tiled=True)  37.3 us
    all_gather x1, waiting for transfers between devices, body(): lax.all_gather(jnp.concatenate(mats, axis=1), ALL, axis=0, tiled=False)  33.6 us
    dot_general x8, matrix products, mm(): return jnp.dot(a, b, preferred_element_type=F32)  26 us
  transfers between devices with their start and end apart: 16, of which 10 were waited for; matrix products, arithmetic and copies ran while one was open for 34% of the time, Pallas kernels for 0%

profile of v1, /device:TPU:0, one launch (start us, length us, event | category | flops | bytes accessed | tf_op | source)
XLA Modules:
  0.0 697.0 jit_solution(13295764174809520821)
XLA Ops:
  8.5 4.0 collective-permute-start.2
  28.4 20.6 %all-gather.5 = bf16[8,96,6]{1,2,0:T(8,128)(2,1)S(1)} all-gather(bf16[1,96,6]{1,2,0:T(8,128)(2,1)S(1)} %bitcast.253), channel_id=1, replica_groups=mesh['fsdp'=2,'ctx'=4,'tp'=4] {'fsdp','ctx'}, dimensions={0}, use_global_device_ids=true | all-gather | bytes 10368 | tf_op jit(solution)/shard_map/all_gather | solution.py:138
  49.2 68.4 %all-gather.4 = bf16[32,3,48]{2,1,0:T(4,128)(2,1)S(1)} all-gather(bf16[1,3,48]{2,1,0:T(4,128)(2,1)S(1)} %maximum_bitcast_fusion.2), channel_id=4, replica_groups=mesh['fsdp'=2,'ctx'=4,'tp'=4] {'fsdp','ctx','tp'}, dimensions={0}, use_global_device_ids=true | all-gather | bytes 9504 | tf_op jit(solution)/shard_map/all_gather | solution.py:139
  127.5 33.6 %all-gather.12.cloned.1.call-done = bf16[3072,2304]{1,0:T(8,128)(2,1)} async-done(((bf16[96,2304]{1,0:T(8,128)(2,1)}), bf16[3072,2304]{1,0:T(8,128)(2,1)}) %all-gather.12.cloned.1.call-update) | async-done | bytes 14155792 | tf_op jit(solution)/shard_map/all_gather | solution.py:129
  161.0 8.1 %fusion.63 = (bf16[32,96,768]{2,1,0:T(8,128)(2,1)}, bf16[32,96,768]{2,1,0:T(8,128)(2,1)}) fusion(bf16[32,96,2304]{2,1,0:T(8,128)(2,1)} %bitcast.193), kind=kLoop, calls=%fused_computation.157 | loop fusion | bytes 18874368 | tf_op jit(solution)/shard_map/slice | solution.py:132
  169.2 7.1 %fusion.64 = (bf16[32,96,192]{2,1,0:T(8,128)(2,1)S(1)}, bf16[32,96,192]{2,1,0:T(8,128)(2,1)S(1)}, bf16[32,96,192]{2,1,0:T(8,128)(2,1)}, bf16[32,96,192]{2,1,0:T(8,128)(2,1)}) fusion(bf16[32,96,2304]{2,1,0:T(8,128)(2,1)} %bitcast.194), kind=kLoop, calls=%fused_computation.158 | loop fusion | bytes 9437184 | tf_op jit(solution)/shard_map/slice | solution.py:132
  179.1 3.8 reshape.349
  191.6 3.8 reshape.355
  215.8 6.1 fusion.69
  222.0 4.1 fusion.25
  233.5 3.8 copy.123
  238.7 3.7 multiply_convert_fusion.1
  248.5 5.0 convert_reduce_fusion
  258.3 4.0 multiply_reduce_fusion
  294.9 19.4 %reduce-scatter.7.cloned.1.call-done = f32[256,1536]{0,1:T(8,128)} async-done(((f32[512,1536]{0,1:T(8,128)}), f32[256,1536]{0,1:T(8,128)}) %reduce-scatter.7.cloned.1.call-update) | async-done | bytes 1572880 | tf_op jit(solution)/shard_map/reduce_scatter | solution.py:211
  318.6 3.9 convolution_convert_fusion.2
  324.4 4.4 reshape.376
  330.4 4.4 reshape.379
  334.8 5.2 convolution_convert_fusion.1
  340.0 9.9 %reshape.380 = bf16[8,96,4,768]{3,2,1,0:T(4,128)(2,1)} reshape(bf16[768,3072]{1,0:T(8,128)(2,1)} %convolution_convert_fusion.1) | data formatting | bytes 9437184 | tf_op jit(solution)/shard_map/reshape | solution.py:223
  350.0 3.6 convolution_convert_fusion
  353.6 9.8 %reshape.381 = bf16[8,96,4,768]{3,2,1,0:T(4,128)(2,1)} reshape(bf16[768,3072]{1,0:T(8,128)(2,1)} %convolution_convert_fusion) | data formatting | bytes 9437184 | tf_op jit(solution)/shard_map/reshape | solution.py:223
  364.9 4.5 reshape.377
  371.0 4.8 reshape.378
  375.8 41.4 %concatenate.27 = bf16[8,4,96,2304]{3,1,2,0:T(4,128)(2,1)} concatenate(bf16[8,4,96,192]{3,1,2,0:T(4,128)(2,1)S(1)} %bitcast.195, bf16[8,4,96,192]{3,1,2,0:T(4,128)(2,1)} %bitcast.197, bf16[8,4,96,192]{3,1,2,0:T(4,128)(2,1)} %bitcast.198, bf16[8,4,96,192]{3,1,2,0:T(4,128)(2,1)S(1)} %bitcast.196, bf16[8,4,96,768]{3,1,2,0:T(4,128)(2,1)} %bitcast.183, bf16[8,4,96,768]{3,1,2,0:T(4,128)(2,1)} %bitcast.184), dimensions={3} | concatenate | bytes 28311552 | tf_op jit(solution)/shard_map/concatenate | solution.py:224
  417.1 11.2 %copy.125 = bf16[8,4,96,2304]{3,2,1,0:T(8,128)(2,1)} copy(bf16[8,4,96,2304]{3,1,2,0:T(4,128)(2,1)} %concatenate.27) | data formatting | bytes 28311552 | tf_op jit(solution)/shard_map/concatenate | solution.py:224
  428.4 3.7 all-to-all-start
  432.1 6.5 all-to-all-done
  438.6 40.9 %all-reduce.3.cloned.1.call-done = f32[32,720]{1,0:T(8,128)} async-done(((f32[32,720]{1,0:T(8,128)}), f32[32,720]{1,0:T(8,128)}) %all-reduce.3.cloned.1.call-update) | async-done | bytes 92176
  481.0 37.2 %reduce-scatter.9.cloned.1.call-done = bf16[4,64,768]{2,1,0:T(8,128)(2,1)} async-done(((bf16[4,256,768]{2,1,0:T(8,128)(2,1)}), bf16[4,64,768]{2,1,0:T(8,128)(2,1)}) %reduce-scatter.9.cloned.1.call-update) | async-done | bytes 393232 | tf_op jit(solution)/shard_map/reduce_scatter | solution.py:91
  523.9 4.1 all-to-all-done.1
  528.1 157.6 %reduce-scatter.11.cloned.1.call-done = bf16[1,96,2304]{2,1,0:T(8,128)(2,1)} async-done(((bf16[32,96,2304]{2,1,0:T(8,128)(2,1)}), bf16[1,96,2304]{2,1,0:T(8,128)(2,1)}) %reduce-scatter.11.cloned.1.call-update) | async-done | bytes 442384 | tf_op jit(solution)/shard_map/reduce_scatter | solution.py:226
  (275 shorter events, 132.1 us)
Async XLA Ops:
  7.2 114.5 %copy-start = (s32[4,1,1024]{2,1,0:T(1,128)S(1)}, s32[4,1,1024]{2,1,0:T(1,128)}, u32[]{:S(2)}) copy-start(s32[4,1,1024]{2,1,0:T(1,128)} %param.22) | copy-start | bytes 49156
  7.2 21.1 %copy-start.54 = (bf16[96]{0:T(256)(128)(2,1)S(1)}, bf16[96]{0:T(256)(128)(2,1)}, u32[]{:S(2)}) copy-start(bf16[96]{0:T(256)(128)(2,1)} %param.29) | copy-start | bytes 580
  7.2 21.1 %copy-start.55 = (bf16[96]{0:T(256)(128)(2,1)S(1)}, bf16[96]{0:T(256)(128)(2,1)}, u32[]{:S(2)}) copy-start(bf16[96]{0:T(256)(128)(2,1)} %param.30) | copy-start | bytes 580
  7.3 21.1 %copy-start.56 = (bf16[96]{0:T(256)(128)(2,1)S(1)}, bf16[96]{0:T(256)(128)(2,1)}, u32[]{:S(2)}) copy-start(bf16[96]{0:T(256)(128)(2,1)} %param.31) | copy-start | bytes 580
  7.3 21.1 %copy-start.57 = (bf16[96]{0:T(256)(128)(2,1)S(1)}, bf16[96]{0:T(256)(128)(2,1)}, u32[]{:S(2)}) copy-start(bf16[96]{0:T(256)(128)(2,1)} %param.35) | copy-start | bytes 580
  7.3 21.1 %copy-start.58 = (bf16[96]{0:T(256)(128)(2,1)S(1)}, bf16[96]{0:T(256)(128)(2,1)}, u32[]{:S(2)}) copy-start(bf16[96]{0:T(256)(128)(2,1)} %param.36) | copy-start | bytes 580
  7.3 21.1 %copy-start.59 = (bf16[96]{0:T(256)(128)(2,1)S(1)}, bf16[96]{0:T(256)(128)(2,1)}, u32[]{:S(2)}) copy-start(bf16[96]{0:T(256)(128)(2,1)} %param.37) | copy-start | bytes 580
  7.3 41.8 %copy-start.51 = (bf16[3,32]{1,0:T(4,128)(2,1)S(1)}, bf16[3,32]{1,0:T(4,128)(2,1)}, u32[]{:S(2)}) copy-start(bf16[3,32]{1,0:T(4,128)(2,1)} %param.33) | copy-start | bytes 580
  7.3 41.8 %copy-start.52 = (bf16[3,8]{1,0:T(4,128)(2,1)S(1)}, bf16[3,8]{1,0:T(4,128)(2,1)}, u32[]{:S(2)}) copy-start(bf16[3,8]{1,0:T(4,128)(2,1)} %param.27) | copy-start | bytes 148
  7.3 41.8 %copy-start.53 = (bf16[3,8]{1,0:T(4,128)(2,1)S(1)}, bf16[3,8]{1,0:T(4,128)(2,1)}, u32[]{:S(2)}) copy-start(bf16[3,8]{1,0:T(4,128)(2,1)} %param.24) | copy-start | bytes 148
  7.3 116.6 %all-gather.10.cloned.1.call-start = ((), (), s32[]{:S(2)}) async-start(), calls=%async_computation.10 | async-start | bytes 1966080 | tf_op jit(solution)/shard_map/all_gather | solution.py:83
  8.5 7.2 %collective-permute-start.2 = (bf16[1,64,768]{2,1,0:T(8,128)(2,1)S(1)}, bf16[1,64,768]{2,1,0:T(8,128)(2,1)S(1)}, u32[]{:S(2)}, u32[]{:S(2)}) collective-permute-start(bf16[1,64,768]{2,1,0:T(8,128)(2,1)S(1)} %get-tuple-element.55), channel_id=1, source_target_pairs={{0,12},{4,8},{8,4},{12,0},{1,13},{5,9},{9,5},{13,1},{2,14},{6,10},... | collective-permute-start | bytes 294920 | tf_op jit(solution)/shard_map/ppermute | solution.py:39
  12.5 4.9 collective-permute-start.1
  13.0 4.7 collective-permute-start
  19.1 141.9 %all-gather.12.cloned.1.call-start = ((), (), s32[]{:S(2)}) async-start(), calls=%async_computation.11 | async-start | bytes 14598144 | tf_op jit(solution)/shard_map/all_gather | solution.py:129
  21.2 223.2 %all-gather.14.cloned.1.call-start = ((), (), s32[]{:S(2)}) async-start(), calls=%async_computation.12 | async-start | bytes 1966080 | tf_op jit(solution)/shard_map/all_gather | solution.py:83
  21.3 101.0 %collective-permute-start.5 = (bf16[1,64,768]{2,1,0:T(8,128)(2,1)S(1)}, bf16[1,64,768]{2,1,0:T(8,128)(2,1)S(1)}, u32[]{:S(2)}, u32[]{:S(2)}) collective-permute-start(bf16[1,64,768]{2,1,0:T(8,128)(2,1)S(1)} %get-tuple-element.51), channel_id=1, source_target_pairs={{0,12},{4,8},{8,4},{12,0},{1,13},{5,9},{9,5},{13,1},{2,14},{6,10},... | collective-permute-start | bytes 294920 | tf_op jit(solution)/shard_map/ppermute | solution.py:39
  22.8 99.5 %collective-permute-start.4 = (bf16[1,64,768]{2,1,0:T(8,128)(2,1)S(1)}, bf16[1,64,768]{2,1,0:T(8,128)(2,1)S(1)}, u32[]{:S(2)}, u32[]{:S(2)}) collective-permute-start(bf16[1,64,768]{2,1,0:T(8,128)(2,1)S(1)} %get-tuple-element.52), channel_id=1, source_target_pairs={{0,8},{4,12},{8,0},{12,4},{1,9},{5,13},{9,1},{13,5},{2,10},{6,14},... | collective-permute-start | bytes 294920 | tf_op jit(solution)/shard_map/ppermute | solution.py:39
  24.3 98.0 %collective-permute-start.3 = (bf16[1,64,768]{2,1,0:T(8,128)(2,1)S(1)}, bf16[1,64,768]{2,1,0:T(8,128)(2,1)S(1)}, u32[]{:S(2)}, u32[]{:S(2)}) collective-permute-start(bf16[1,64,768]{2,1,0:T(8,128)(2,1)S(1)} %get-tuple-element.50), channel_id=1, source_target_pairs={{0,4},{4,0},{8,12},{12,8},{1,5},{5,1},{9,13},{13,9},{2,6},{6,2},{1... | collective-permute-start | bytes 294920 | tf_op jit(solution)/shard_map/ppermute | solution.py:39
  123.7 190.6 %reduce-scatter.7.cloned.1.call-start = ((), (), s32[]{:S(2)}) async-start(), calls=%async_computation.7 | async-start | bytes 4718592 | tf_op jit(solution)/shard_map/reduce_scatter | solution.py:211
  226.7 29.1 %copy-start.2 = (f32[256,768]{1,0:T(8,128)}, f32[256,768]{1,0:T(8,128)S(1)}, u32[]{:S(2)}) copy-start(f32[256,768]{1,0:T(8,128)S(1)} %get-tuple-element.70) | copy-start | bytes 2359300
  272.1 156.3 %reduce-scatter.5.cloned.1.call-start = ((), (), s32[]{:S(2)}) async-start(), calls=%async_computation.6 | async-start | bytes 1966080 | tf_op jit(solution)/shard_map/reduce_scatter | solution.py:91
  275.3 204.2 %all-reduce.3.cloned.1.call-start = ((), (), s32[]{:S(2)}) async-start(), calls=%async_computation.13 | async-start | bytes 196608
  292.6 23.6 %copy-start.29 = (f32[8,4,3,32]{3,1,0,2:T(4,128)S(1)}, f32[8,4,3,32]{3,1,0,2:T(4,128)}, u32[]{:S(2)}) copy-start(f32[8,4,3,32]{3,1,0,2:T(4,128)} %copy.128) | copy-start | bytes 36868
  292.7 23.7 %copy-start.28 = (f32[32,576]{1,0:T(8,128)S(1)}, f32[32,576]{1,0:T(8,128)}, u32[]{:S(2)}) copy-start(f32[32,576]{1,0:T(8,128)} %reshape.390) | copy-start | bytes 221188
  292.7 24.4 %copy-start.13 = (bf16[768,768]{0,1:T(8,128)(2,1)S(1)}, bf16[768,768]{0,1:T(8,128)(2,1)}, u32[]{:S(2)}) copy-start(bf16[768,768]{0,1:T(8,128)(2,1)} %copy-done.12) | copy-start | bytes 3538948
  294.9 23.7 %copy-start.45 = (s32[256]{0:T(256)S(1)}, s32[256]{0:T(256)}, u32[]{:S(2)}) copy-start(s32[256]{0:T(256)} %dynamic_slice.37) | copy-start | bytes 3076
  318.5 199.6 %reduce-scatter.9.cloned.1.call-start = ((), (), s32[]{:S(2)}) async-start(), calls=%async_computation.8 | async-start | bytes 1966080 | tf_op jit(solution)/shard_map/reduce_scatter | solution.py:91
  322.5 363.1 %reduce-scatter.11.cloned.1.call-start = ((), (), s32[]{:S(2)}) async-start(), calls=%async_computation.9 | async-start | bytes 14598144 | tf_op jit(solution)/shard_map/reduce_scatter | solution.py:226
  428.4 261.5 %copy-start.1 = (s32[4,1,1024]{2,1,0:T(1,128)S(1)}, s32[4,1,1024]{2,1,0:T(1,128)}, u32[]{:S(2)}) copy-start(s32[4,1,1024]{2,1,0:T(1,128)} %param.22) | copy-start | bytes 49156
  428.4 10.2 %all-to-all-start = ((bf16[4,64,768]{2,1,0:T(8,128)(2,1)}), bf16[4,64,768]{2,1,0:T(8,128)(2,1)S(1)}, u32[]{:S(2)}, u32[]{:S(2)}) async-start(bf16[4,64,768]{2,1,0:T(8,128)(2,1)} %reduce-scatter.5.cloned.1.call-done), calls=%async_computation.1 | async-start | bytes 786432 | tf_op jit(solution)/shard_map/all_to_all | solution.py:92
  518.2 9.9 %all-to-all-start.1 = ((bf16[4,64,768]{2,1,0:T(8,128)(2,1)}), bf16[4,64,768]{2,1,0:T(8,128)(2,1)S(1)}, u32[]{:S(2)}, u32[]{:S(2)}) async-start(bf16[4,64,768]{2,1,0:T(8,128)(2,1)} %reduce-scatter.9.cloned.1.call-done), calls=%async_computation.4 | async-start | bytes 786432 | tf_op jit(solution)/shard_map/all_to_all | solution.py:92
  (50 other events, 270.8 us)
Sparse Core Ops, SparseCore 0:
  19.3 37.4 all-gather.9
  59.5 101.4 all-gather.11
  162.6 35.4 all-gather.13
  272.3 42.0 reduce-scatter.6
  316.5 35.4 reduce-scatter.4
  358.0 121.4 all-reduce.2
  481.8 36.3 reduce-scatter.8
  524.2 161.4 reduce-scatter.10
